TPU v7x, 32 devices: a whole 2x2x4 slice. The times are simulated.
32 devices in a mesh: fsdp: 4 (over y, x), tenant: 4 (over z), dp: 2 (over core).
Axes of the slice: x: 2, y: 2, z: 4, core: 2. Of those that a mesh axis runs over, the one named last changes fastest.
Arguments:
- tokens: bfloat16 [3072, 5120], P(('fsdp', 'dp'), 'tenant'), may hold values from -6 to 6
- block_tenant_index: int32 [48], P(('fsdp', 'dp')), may hold values from 0 to 7
- ranks: int32 [8], replicated, may hold values from 16 to 64, as said below
- frozen_up_weight: bfloat16 [5120, 14336], P(('fsdp', 'dp'), 'tenant'), may hold values from -0.078125 to 0.078125
- tenant_down_adapters: bfloat16 [8, 64, 5120], P('tenant'), may hold values from -0.078125 to 0.078125
- tenant_up_adapters: bfloat16 [8, 64, 14336], P('tenant'), may hold values from -0.75 to 0.75
- cotangent: bfloat16 [3072, 14336], P(('fsdp', 'dp'), 'tenant'), may hold values from -6 to 6
Outputs:
- hidden_out: bfloat16 [3072, 14336], P(('fsdp', 'dp'), 'tenant')
- grad_tokens: bfloat16 [3072, 5120], P(('fsdp', 'dp'), 'tenant')
- grad_down: float32 [8, 64, 5120], P('dp', None, 'tenant')
- grad_up: float32 [8, 64, 14336], P('dp', None, 'tenant')
Inputs may be any that keep to these rules, and one draw needn't show every extreme that they name: `ranks`: multiples of 16; some tenant has rank 64.
All inputs are finite; a program needn't handle non-finite values.
Results may differ from a plain program's by a relative error of at most 0.0034.
Values may be sent and summed in bfloat16 or wider, within the bound.
A program may use at most 128 MiB of HBM per device.

v0:
```python
import jax
import jax.numpy as jnp
from jax import lax
from jax.sharding import PartitionSpec as P

BLOCK = 64
alpha_scale = 32.0
BF16 = jnp.bfloat16
F32 = jnp.float32


def nt(a, b):
    return lax.dot_general(a, b, (((1,), (1,)), ((), ())), preferred_element_type=F32)


def tn(a, b):
    return lax.dot_general(a, b, (((0,), (0,)), ((), ())), preferred_element_type=F32)


def fetch_adapter(adapter, tenant_n, dp_n):
    share = adapter.shape[1] // dp_n
    mine = lax.dynamic_slice_in_dim(adapter, lax.axis_index("dp") * share, share, axis=1)
    part = lax.all_to_all(mine, "tenant", split_axis=2, concat_axis=0, tiled=True)
    return lax.all_gather(part, "dp", axis=1, tiled=True)


def reduce_fsdp(x, fsdp_n):
    rows = x.shape[0]
    got = lax.all_to_all(
        x.astype(BF16).reshape(fsdp_n, rows // fsdp_n, x.shape[1]), "fsdp", 0, 0, tiled=True
    )
    total = jnp.sum(got.astype(F32), axis=0).astype(BF16)
    return lax.all_gather(total, "fsdp", axis=0, tiled=True).astype(F32)


def make_shards(mesh):
    tenant_n, fsdp_n, dp_n = (mesh.shape["tenant"], mesh.shape["fsdp"], mesh.shape["dp"])

    def shards(
        tokens,
        block_tenant_index,
        ranks,
        frozen_up_weight,
        tenant_down_adapters,
        tenant_up_adapters,
        cotangent,
    ):
        rows, local_d = tokens.shape
        local_f = cotangent.shape[1]
        tenants = ranks.shape[0]
        rank = tenant_down_adapters.shape[1]
        depth = frozen_up_weight.shape[0]
        blocks = fsdp_n * dp_n
        first = max(128, depth * 3 // 5 // 128 * 128) if depth > 128 else depth
        cuts = [(0, first)] + ([(first, depth)] if first < depth else [])
        weights = [
            lax.all_gather(frozen_up_weight[a:b], ("fsdp", "dp"), axis=0, tiled=True)
            for a, b in cuts
        ]
        up = fetch_adapter(tenant_up_adapters, tenant_n, dp_n).reshape(tenants * rank, local_f)
        down = fetch_adapter(tenant_down_adapters, tenant_n, dp_n).reshape(tenants * rank, local_d)
        onehot = block_tenant_index[:, None] == jnp.arange(tenants, dtype=jnp.int32)[None, :]
        sel = onehot.astype(F32)[:, None, :, None]
        own_rank = jnp.sum(jnp.where(onehot, ranks[None, :], 0), axis=1)
        keep = jnp.arange(rank, dtype=jnp.int32)[None, :] < own_rank[:, None]
        gain = jnp.where(keep, (alpha_scale / own_rank.astype(F32))[:, None], F32(0.0))

        def compact(full):
            full = full.reshape(rows // BLOCK, BLOCK, tenants, rank)
            return jnp.sum(full * sel, axis=2)

        both = jnp.concatenate([compact(nt(tokens, down)), compact(nt(cotangent, up))], axis=2)
        both = lax.psum(both, "tenant")

        def spread(values):
            scaled = (values * gain[:, None, :]).astype(BF16)
            return (scaled[:, :, None, :] * sel.astype(BF16)).reshape(rows, tenants * rank)

        adapted = spread(both[:, :, :rank])
        adapted_grad = spread(both[:, :, rank:])
        terms = jnp.concatenate([tn(adapted, cotangent), tn(adapted_grad, tokens)], axis=1)
        terms = lax.psum_scatter(terms, "dp", scatter_dimension=0, tiled=True)
        grads = reduce_fsdp(terms, fsdp_n)
        grad_up = grads[:, :local_f].reshape(tenants // dp_n, rank, local_f)
        grad_down = grads[:, local_f:].reshape(tenants // dp_n, rank, local_d)
        whole = lax.all_gather(tokens, "tenant", axis=1, tiled=True)
        whole3 = whole.reshape(rows, blocks, depth)
        hidden = jnp.dot(adapted, up, preferred_element_type=F32)
        pieces = []
        for (a, b), weight in zip(cuts, weights):
            back = nt(cotangent, weight).astype(BF16)
            n = b - a
            got = lax.all_to_all(
                back.reshape(rows, tenant_n, blocks * n // tenant_n).transpose(1, 0, 2),
                "tenant",
                0,
                0,
                tiled=True,
            )
            pieces.append(jnp.sum(got.astype(F32), axis=0).reshape(rows, blocks // tenant_n, n))
            hidden = hidden + jnp.dot(
                whole3[:, :, a:b].reshape(rows, blocks * n), weight, preferred_element_type=F32
            )
        hidden_out = hidden.astype(BF16)
        grad_base = jnp.concatenate(pieces, axis=2).reshape(rows, local_d)
        grad_tokens = (grad_base + jnp.dot(adapted_grad, down, preferred_element_type=F32)).astype(
            BF16
        )
        return (hidden_out, grad_tokens, grad_down, grad_up)

    return shards


def solution(mesh):
    return jax.shard_map(
        make_shards(mesh),
        mesh=mesh,
        in_specs=(
            P(("fsdp", "dp"), "tenant"),
            P(("fsdp", "dp")),
            P(),
            P(("fsdp", "dp"), "tenant"),
            P("tenant", None, None),
            P("tenant", None, None),
            P(("fsdp", "dp"), "tenant"),
        ),
        out_specs=(
            P(("fsdp", "dp"), "tenant"),
            P(("fsdp", "dp"), "tenant"),
            P("dp", None, "tenant"),
            P("dp", None, "tenant"),
        ),
        check_vma=False,
    )
```

profile of v0, /device:TPU:0, one launch (start us, length us, event | category | flops | bytes accessed | tf_op | source)
XLA Modules:
  0.0 595.5 jit_solution(8852192433115120866)
XLA Ops:
  8.5 4.0 copy.30
  12.5 4.9 reshape.171
  17.4 6.3 %all-to-all-start = ((bf16[4,2,40960]{2,1,0:T(2,128)(2,1)}), bf16[4,2,40960]{2,1,0:T(2,128)(2,1)S(1)}, u32[]{:S(2)}, u32[]{:S(2)}) async-start(bf16[4,2,40960]{2,1,0:T(2,128)(2,1)} %reshape.171), calls=%async_computation | async-start | bytes 1310720 | tf_op jit(solution)/shard_map/all_to_all | solution.py:23
  23.8 2.8 constant_dynamic-slice_fusion
  26.6 15.2 %copy.31 = bf16[2,32,14336]{1,0,2:T(2,128)(2,1)} copy(bf16[2,32,14336]{2,1,0:T(8,128)(2,1)} %constant_dynamic-slice_fusion) | data formatting | bytes 3670016
  41.9 9.4 %reshape.173 = bf16[4,2,114688]{2,1,0:T(2,128)(2,1)} reshape(bf16[14336,2,32]{2,1,0:T(2,128)(2,1)} %bitcast.65) | data formatting | bytes 3670016
  51.3 5.1 all-to-all-start.1
  56.4 2.6 reshape.172
  59.0 6.2 %copy.28 = bf16[2,32,4,1280]{3,2,1,0:T(4,128)(2,1)S(1)} copy(bf16[2,32,4,1280]{1,0,3,2:T(2,128)(2,1)} %bitcast.70) | data formatting | bytes 1310720 | tf_op jit(solution)/shard_map/all_to_all | solution.py:23
  66.2 32.3 %all-to-all-done.1 = bf16[4,2,114688]{2,1,0:T(2,128)(2,1)} async-done(((bf16[4,2,114688]{2,1,0:T(2,128)(2,1)}), bf16[4,2,114688]{2,1,0:T(2,128)(2,1)}, u32[]{:S(2)}, u32[]{:S(2)}) %all-to-all-start.1) | async-done | bytes 1835040 | tf_op jit(solution)/shard_map/all_to_all | solution.py:23
  98.5 6.9 %reshape.174 = bf16[14336,2,32]{2,1,0:T(2,128)(2,1)} reshape(bf16[4,2,114688]{2,1,0:T(2,128)(2,1)} %all-to-all-done.1) | data formatting | bytes 3670016
  105.4 18.1 %copy.29 = bf16[2,32,4,3584]{3,2,1,0:T(4,128)(2,1)} copy(bf16[2,32,4,3584]{1,0,3,2:T(2,128)(2,1)} %bitcast.66) | data formatting | bytes 3670016 | tf_op jit(solution)/shard_map/all_to_all | solution.py:23
  123.5 3.0 copy.24
  126.7 3.3 convolution_bitcast_fusion.1
  132.9 5.8 all-gather.9.cloned.1.call-done
  138.7 5.0 convolution_bitcast_fusion
  146.6 2.9 multiply_reduce_fusion.1
  151.4 35.2 %all-reduce.2.cloned.1.call-done = f32[6,64,128]{2,1,0:T(8,128)} async-done(((f32[6,64,128]{2,1,0:T(8,128)}), f32[6,64,128]{2,1,0:T(8,128)}) %all-reduce.2.cloned.1.call-update) | async-done | bytes 196624 | tf_op jit(solution)/shard_map/psum | solution.py:73
  189.2 1.7 mul.91
  190.9 1.8 mul.87
  192.7 3.6 fusion.11
  196.3 5.0 fusion.10
  201.3 8.3 %pad_maximum_fusion = f32[512,4864]{1,0:T(8,128)} fusion(f32[512,1280]{1,0:T(8,128)} %fusion.11, f32[512,3584]{1,0:T(8,128)} %fusion.10), kind=kLoop, calls=%fused_computation | loop fusion | flops 2490368 | bytes 19922944 | tf_op jit(solution)/shard_map/concatenate | solution.py:81
  209.7 2.9 slice.28
  212.6 3.5 slice.26
  216.2 48.0 %all-gather.11.cloned.1.call-done = bf16[384,5120]{1,0:T(8,128)(2,1)} async-done(((bf16[384,1280]{1,0:T(8,128)(2,1)}), bf16[384,5120]{1,0:T(8,128)(2,1)}) %all-gather.11.cloned.1.call-update) | async-done | bytes 3932176 | tf_op jit(solution)/shard_map/all_gather | solution.py:86
  264.2 2.9 copy.34
  267.5 1.9 copy.35
  271.1 11.4 %reduce-scatter.2.cloned.1.call-done = f32[256,4864]{1,0:T(8,128)} async-done(((f32[512,4864]{1,0:T(8,128)}), f32[256,4864]{1,0:T(8,128)}) %reduce-scatter.2.cloned.1.call-update) | async-done | bytes 4980752 | tf_op jit(solution)/shard_map/reduce_scatter | solution.py:82
  282.5 4.1 convert_element_type.69
  286.6 4.6 all-to-all-start.4
  291.2 6.6 %fusion.8 = f32[384,3584]{1,0:T(8,128)} fusion(bf16[384,512]{1,0:T(8,128)(2,1)S(1)} %mul.87, bf16[512,3584]{1,0:T(8,128)(2,1)} %bitcast.82), kind=kOutput, calls=%fused_computation.33 | convolution fusion | flops 1409286144 | bytes 9568256 | tf_op jit(solution)/shard_map/dot_general | solution.py:88
  297.8 92.3 %all-gather.15.cloned.1.call-done = bf16[2048,3584]{1,0:T(8,128)(2,1)} async-done(((bf16[256,3584]{1,0:T(8,128)(2,1)}), bf16[2048,3584]{1,0:T(8,128)(2,1)}) %all-gather.15.cloned.1.call-update) | async-done | bytes 14680080 | tf_op jit(solution)/shard_map/all_gather | solution.py:57
  390.1 9.4 %convolution_convert_fusion.1 = bf16[384,2048]{1,0:T(8,128)(2,1)S(1)} fusion(bf16[384,3584]{1,0:T(8,128)(2,1)S(1)} %copy-done, bf16[2048,3584]{1,0:T(8,128)(2,1)} %all-gather.15.cloned.1.call-done), kind=kOutput, calls=%fused_computation.9 | convolution fusion | flops 5637931008 | bytes 19005440 | tf_op jit(solution)/shard_map/dot_general | solution.py:13
  400.9 4.6 all-to-all-start.3
  405.5 3.1 reduce_sum.62
  408.6 95.9 %all-gather.13.cloned.1.call-done = bf16[3072,3584]{1,0:T(8,128)(2,1)} async-done(((bf16[384,3584]{1,0:T(8,128)(2,1)}), bf16[3072,3584]{1,0:T(8,128)(2,1)}) %all-gather.13.cloned.1.call-update) | async-done | bytes 22020112 | tf_op jit(solution)/shard_map/all_gather | solution.py:57
  504.5 14.0 %convolution_convert_fusion = bf16[384,3072]{1,0:T(8,128)(2,1)} fusion(bf16[384,3584]{1,0:T(8,128)(2,1)S(1)} %copy-done, bf16[3072,3584]{1,0:T(8,128)(2,1)} %all-gather.13.cloned.1.call-done), kind=kOutput, calls=%fused_computation.5 | convolution fusion | flops 8456896512 | bytes 27131904 | tf_op jit(solution)/shard_map/dot_general | solution.py:13
  518.6 3.2 copy.40
  521.8 4.7 all-to-all-start.2
  526.5 11.6 %fusion.9 = f32[384,3584]{1,0:T(8,128)} fusion(bf16[384,2048]{1,0:T(8,128)(2,1)S(1)} %bitcast.87, bf16[2048,3584]{1,0:T(8,128)(2,1)} %all-gather.15.cloned.1.call-done), kind=kOutput, calls=%fused_computation.34 | convolution fusion | flops 5637144576 | bytes 21757952 | tf_op jit(solution)/shard_map/dot_general | solution.py:101
  541.2 4.2 all-gather.17.cloned.1.call-done
  545.4 2.4 slice.36
  547.8 2.3 slice.37
  550.1 18.7 %fusion.1 = bf16[384,3584]{1,0:T(8,128)(2,1)} fusion(f32[384,3584]{1,0:T(8,128)} %fusion.9, f32[384,3584]{1,0:T(8,128)} %fusion.8, bf16[384,3072]{1,0:T(8,128)(2,1)S(1)} %bitcast.85, bf16[3072,3584]{1,0:T(8,128)(2,1)} %all-gather.13.cloned.1.call-done), kind=kOutput, calls=%fused_computation.3 | convolution fusion | flops 8459845632 | bytes 38141952 | tf_op jit(solution)/shard_map/dot_general | solution.py:101
  568.8 12.2 %all-to-all-done.2 = bf16[4,384,768]{2,1,0:T(8,128)(2,1)} async-done(((bf16[4,384,768]{2,1,0:T(8,128)(2,1)}), bf16[4,384,768]{2,1,0:T(8,128)(2,1)}, u32[]{:S(2)}, u32[]{:S(2)}) %all-to-all-start.2) | async-done | bytes 2359328 | tf_op jit(solution)/shard_map/all_to_all | solution.py:93
  581.0 2.1 convert_reduce_fusion
  583.8 2.0 pad_maximum_fusion.1
  (58 shorter events, 22.7 us)
Async XLA Ops:
  7.2 131.6 %copy-start = (bf16[384,3584]{1,0:T(8,128)(2,1)S(1)}, bf16[384,3584]{1,0:T(8,128)(2,1)}, u32[]{:S(2)}) copy-start(bf16[384,3584]{1,0:T(8,128)(2,1)} %param.13) | copy-start | bytes 8257540
  17.4 33.8 %all-to-all-start = ((bf16[4,2,40960]{2,1,0:T(2,128)(2,1)}), bf16[4,2,40960]{2,1,0:T(2,128)(2,1)S(1)}, u32[]{:S(2)}, u32[]{:S(2)}) async-start(bf16[4,2,40960]{2,1,0:T(2,128)(2,1)} %reshape.171), calls=%async_computation | async-start | bytes 1310720 | tf_op jit(solution)/shard_map/all_to_all | solution.py:23
  51.3 47.2 %all-to-all-start.1 = ((bf16[4,2,114688]{2,1,0:T(2,128)(2,1)}), bf16[4,2,114688]{2,1,0:T(2,128)(2,1)}, u32[]{:S(2)}, u32[]{:S(2)}) async-start(bf16[4,2,114688]{2,1,0:T(2,128)(2,1)} %reshape.173), calls=%async_computation.1 | async-start | bytes 3670016 | tf_op jit(solution)/shard_map/all_to_all | solution.py:23
  56.4 70.4 %all-gather.7.cloned.1.call-start = ((), (), s32[]{:S(2)}) async-start(), calls=%async_computation.6 | async-start | bytes 1966080 | tf_op jit(solution)/shard_map/all_gather | solution.py:24
  66.1 72.6 %all-gather.9.cloned.1.call-start = ((), (), s32[]{:S(2)}) async-start(), calls=%async_computation.7 | async-start | bytes 5505024 | tf_op jit(solution)/shard_map/all_gather | solution.py:24
  123.5 3.1 copy-start.6
  126.6 60.1 %all-reduce.2.cloned.1.call-start = ((), (), s32[]{:S(2)}) async-start(), calls=%async_computation.8 | async-start | bytes 393216 | tf_op jit(solution)/shard_map/psum | solution.py:73
  146.6 4.6 copy-start.7
  150.3 113.9 %all-gather.11.cloned.1.call-start = ((), (), s32[]{:S(2)}) async-start(), calls=%async_computation.9 | async-start | bytes 4915200 | tf_op jit(solution)/shard_map/all_gather | solution.py:86
  150.9 131.6 %reduce-scatter.2.cloned.1.call-start = ((), (), s32[]{:S(2)}) async-start(), calls=%async_computation.12 | async-start | bytes 14942208 | tf_op jit(solution)/shard_map/reduce_scatter | solution.py:82
  209.6 180.5 %all-gather.15.cloned.1.call-start = ((), (), s32[]{:S(2)}) async-start(), calls=%async_computation.11 | async-start | bytes 16515072 | tf_op jit(solution)/shard_map/all_gather | solution.py:57
  212.6 291.9 %all-gather.13.cloned.1.call-start = ((), (), s32[]{:S(2)}) async-start(), calls=%async_computation.10 | async-start | bytes 24772608 | tf_op jit(solution)/shard_map/all_gather | solution.py:57
  286.6 114.2 %all-to-all-start.4 = ((bf16[4,64,4864]{2,1,0:T(8,128)(2,1)}), bf16[4,64,4864]{2,1,0:T(8,128)(2,1)}, u32[]{:S(2)}, u32[]{:S(2)}) async-start(bf16[4,64,4864]{2,1,0:T(8,128)(2,1)} %bitcast.71), calls=%async_computation.5 | async-start | bytes 4980736 | tf_op jit(solution)/shard_map/all_to_all | solution.py:29
  400.9 120.9 %all-to-all-start.3 = ((bf16[4,384,512]{2,1,0:T(8,128)(2,1)}), bf16[4,384,512]{2,1,0:T(8,128)(2,1)}, u32[]{:S(2)}, u32[]{:S(2)}) async-start(bf16[4,384,512]{2,1,0:T(8,128)(2,1)} %bitcast.77), calls=%async_computation.3 | async-start | bytes 3145728 | tf_op jit(solution)/shard_map/all_to_all | solution.py:93
  405.5 139.9 %all-gather.17.cloned.1.call-start = ((), (), s32[]{:S(2)}) async-start(), calls=%async_computation.13 | async-start | bytes 3112960 | tf_op jit(solution)/shard_map/all_gather | solution.py:33
  521.8 4.7 copy-start.4
  521.8 59.2 %all-to-all-start.2 = ((bf16[4,384,768]{2,1,0:T(8,128)(2,1)}), bf16[4,384,768]{2,1,0:T(8,128)(2,1)}, u32[]{:S(2)}, u32[]{:S(2)}) async-start(bf16[4,384,768]{2,1,0:T(8,128)(2,1)} %bitcast.62), calls=%async_computation.2 | async-start | bytes 4718592 | tf_op jit(solution)/shard_map/all_to_all | solution.py:93
  545.4 2.4 copy-start.2
  547.8 2.3 copy-start.3
  585.8 1.3 copy-start.5
  585.8 2.9 copy-start.1
Sparse Core Ops, SparseCore 0:
  66.2 10.8 all-gather.6
  126.7 11.9 all-gather.8
  150.5 36.1 all-reduce.1
  188.1 76.0 all-gather.10
  266.4 16.1 reduce-scatter.1
  284.3 105.8 all-gather.14
  392.6 111.8 all-gather.12
  506.9 38.4 all-gather.16
where the time goes:
time: 598 us; the launch traced here: 596 us
  waiting for transfers between devices  338 us (57%)
  local copies, waits for them, and re-layouts  111 us (19%)
  matrix products  79 us (13%)
  other arithmetic  27.8 us (5%)
  starting transfers between devices  25.8 us (4%)
  between operations  14.3 us (2%)
    all_gather x2, waiting for transfers between devices, shards(): lax.all_gather(frozen_up_weight[a:b], ('fsdp', 'dp'), axis=0, tiled=True)  188 us
    unnamed x26, local copies, waits for them, and re-layouts  51 us
    all_gather x1, waiting for transfers between devices, shards(): whole = lax.all_gather(tokens, 'tenant', axis=1, tiled=True)  48 us
    psum x1, waiting for transfers between devices, shards(): both = lax.psum(both, 'tenant')  35.2 us
    all_to_all x2, waiting for transfers between devices, fetch_adapter(): lax.all_to_all(mine, 'tenant', split_axis=2, concat_axis=0, tiled=True)  32.3 us
    dot_general x4, matrix products, nt(): lax.dot_general(a, b, (((1,), (1,)), ((), ())), preferred_element_type=F32)  31.8 us
    dot_general x2, matrix products, shards(): jnp.dot(whole3[:, :, a:b].reshape(rows, blocks * n), weight, preferred_el...  30.3 us
    all_to_all x4, local copies, waits for them, and re-layouts, fetch_adapter(): lax.all_to_all(mine, 'tenant', split_axis=2, concat_axis=0, tiled=True)  28.3 us
  transfers between devices with their start and end apart: 13, of which 9 were waited for; matrix products, arithmetic and copies ran while one was open for 32% of the time, Pallas kernels for 0%

commit v1 on v0

--- a/solution.py
+++ b/solution.py
@@ -1,12 +1,21 @@
+import functools
 import jax
 import jax.numpy as jnp
 from jax import lax
 from jax.sharding import PartitionSpec as P
+from jax.lax import all_gather
 
 BLOCK = 64
 alpha_scale = 32.0
 BF16 = jnp.bfloat16
 F32 = jnp.float32
+
+
+def review_set(t0, peer_axis):
+    return jnp.concatenate(all_gather(t0, peer_axis), axis=1)
+
+
+choose_the_cycles = functools.partial(review_set, peer_axis="tenant")
 
 
 def nt(a, b):
@@ -83,7 +92,7 @@
         grads = reduce_fsdp(terms, fsdp_n)
         grad_up = grads[:, :local_f].reshape(tenants // dp_n, rank, local_f)
         grad_down = grads[:, local_f:].reshape(tenants // dp_n, rank, local_d)
-        whole = lax.all_gather(tokens, "tenant", axis=1, tiled=True)
+        whole = choose_the_cycles(tokens)
         whole3 = whole.reshape(rows, blocks, depth)
         hidden = jnp.dot(adapted, up, preferred_element_type=F32)
         pieces = []

time: 598 us -> 596 us (level)
  matrix products: 79 us -> 71.2 us
    all_gather x2, waiting for transfers between devices: 188 us -> 164 us  [shards(): lax.all_gather(frozen_up_weight[a:b], ('fsdp', 'dp'), axis=0, tiled=True)]
    all_gather x1, waiting for transfers between devices: 48 us -> 70.5 us  [review_set(): return jnp.concatenate(all_gather(t0, peer_axis), axis=1)]
    unnamed x26 -> x29, local copies, waits for them, and re-layouts: 51 us -> 44.4 us
    reshape x0 -> x1, local copies, waits for them, and re-layouts: none -> 6.26 us  [review_set(): return jnp.concatenate(all_gather(t0, peer_axis), axis=1)]
    slice x2, local copies, waits for them, and re-layouts: 0.34 us -> 6.47 us  [shards(): whole3[:, :, a:b].reshape(rows, blocks * n)]
  transfers between devices with their start and end apart: 13 -> 13, of which waited for: 9 -> 9; matrix products, arithmetic and copies ran while one was open for 32% -> 27% of each run, Pallas kernels for 0% -> 0%
where the time goes in v1:
time: 596 us; the launch traced here: 593 us
  waiting for transfers between devices  337 us (57%)
  local copies, waits for them, and re-layouts  116 us (19%)
  matrix products  71.2 us (12%)
  other arithmetic  27.8 us (5%)
  starting transfers between devices  25.8 us (4%)
  between operations  14.3 us (2%)
    all_gather x2, waiting for transfers between devices, shards(): lax.all_gather(frozen_up_weight[a:b], ('fsdp', 'dp'), axis=0, tiled=True)  164 us
    all_gather x1, waiting for transfers between devices, review_set(): return jnp.concatenate(all_gather(t0, peer_axis), axis=1)  70.5 us
    unnamed x29, local copies, waits for them, and re-layouts  44.4 us
    psum x1, waiting for transfers between devices, shards(): both = lax.psum(both, 'tenant')  36.1 us
    all_to_all x2, waiting for transfers between devices, fetch_adapter(): lax.all_to_all(mine, 'tenant', split_axis=2, concat_axis=0, tiled=True)  32.3 us
    dot_general x4, matrix products, nt(): lax.dot_general(a, b, (((1,), (1,)), ((), ())), preferred_element_type=F32)  31.8 us
    all_to_all x4, local copies, waits for them, and re-layouts, fetch_adapter(): lax.all_to_all(mine, 'tenant', split_axis=2, concat_axis=0, tiled=True)  28.3 us
    dot_general x2, matrix products, shards(): jnp.dot(whole3[:, :, a:b].reshape(rows, blocks * n), weight, preferred_el...  25.9 us
  transfers between devices with their start and end apart: 13, of which 9 were waited for; matrix products, arithmetic and copies ran while one was open for 27% of the time, Pallas kernels for 0%

profile of v1, /device:TPU:0, one launch (start us, length us, event | category | flops | bytes accessed | tf_op | source)
XLA Modules:
  0.0 592.7 jit_solution(8914918592966045438)
XLA Ops:
  8.5 4.0 copy.32
  12.5 4.9 reshape.172
  17.4 6.3 %all-to-all-start = ((bf16[4,2,40960]{2,1,0:T(2,128)(2,1)}), bf16[4,2,40960]{2,1,0:T(2,128)(2,1)S(1)}, u32[]{:S(2)}, u32[]{:S(2)}) async-start(bf16[4,2,40960]{2,1,0:T(2,128)(2,1)} %reshape.172), calls=%async_computation | async-start | bytes 1310720 | tf_op jit(solution)/shard_map/all_to_all | solution.py:32
  23.8 2.8 constant_dynamic-slice_fusion
  26.6 15.2 %copy.33 = bf16[2,32,14336]{1,0,2:T(2,128)(2,1)} copy(bf16[2,32,14336]{2,1,0:T(8,128)(2,1)} %constant_dynamic-slice_fusion) | data formatting | bytes 3670016
  41.9 9.4 %reshape.174 = bf16[4,2,114688]{2,1,0:T(2,128)(2,1)} reshape(bf16[14336,2,32]{2,1,0:T(2,128)(2,1)} %bitcast.67) | data formatting | bytes 3670016
  51.3 5.1 all-to-all-start.1
  56.4 2.6 reshape.173
  59.0 6.2 %copy.30 = bf16[2,32,4,1280]{3,2,1,0:T(4,128)(2,1)S(1)} copy(bf16[2,32,4,1280]{1,0,3,2:T(2,128)(2,1)} %bitcast.72) | data formatting | bytes 1310720 | tf_op jit(solution)/shard_map/all_to_all | solution.py:32
  66.2 32.3 %all-to-all-done.1 = bf16[4,2,114688]{2,1,0:T(2,128)(2,1)} async-done(((bf16[4,2,114688]{2,1,0:T(2,128)(2,1)}), bf16[4,2,114688]{2,1,0:T(2,128)(2,1)}, u32[]{:S(2)}, u32[]{:S(2)}) %all-to-all-start.1) | async-done | bytes 1835040 | tf_op jit(solution)/shard_map/all_to_all | solution.py:32
  98.5 6.8 %reshape.175 = bf16[14336,2,32]{2,1,0:T(2,128)(2,1)} reshape(bf16[4,2,114688]{2,1,0:T(2,128)(2,1)} %all-to-all-done.1) | data formatting | bytes 3670016
  105.3 18.1 %copy.31 = bf16[2,32,4,3584]{3,2,1,0:T(4,128)(2,1)} copy(bf16[2,32,4,3584]{1,0,3,2:T(2,128)(2,1)} %bitcast.68) | data formatting | bytes 3670016 | tf_op jit(solution)/shard_map/all_to_all | solution.py:32
  123.5 3.1 copy.25
  126.9 3.3 convolution_bitcast_fusion.1
  133.1 5.6 all-gather.10.cloned.1.call-done
  138.7 5.0 convolution_bitcast_fusion
  146.6 2.9 multiply_reduce_fusion.1
  150.6 36.1 %all-reduce.2.cloned.1.call-done = f32[6,64,128]{2,1,0:T(8,128)} async-done(((f32[6,64,128]{2,1,0:T(8,128)}), f32[6,64,128]{2,1,0:T(8,128)}) %all-reduce.2.cloned.1.call-update) | async-done | bytes 196624 | tf_op jit(solution)/shard_map/psum | solution.py:82
  190.9 1.8 mul.87
  192.7 3.6 fusion.11
  196.2 5.0 fusion.10
  201.3 8.3 %pad_maximum_fusion = f32[512,4864]{1,0:T(8,128)} fusion(f32[512,1280]{1,0:T(8,128)} %fusion.11, f32[512,3584]{1,0:T(8,128)} %fusion.10), kind=kLoop, calls=%fused_computation | loop fusion | flops 2490368 | bytes 19922944 | tf_op jit(solution)/shard_map/concatenate | solution.py:90
  210.2 2.9 slice.28
  213.2 3.5 slice.26
  216.7 10.3 %reduce-scatter.2.cloned.1.call-done = f32[256,4864]{1,0:T(8,128)} async-done(((f32[512,4864]{1,0:T(8,128)}), f32[256,4864]{1,0:T(8,128)}) %reduce-scatter.2.cloned.1.call-update) | async-done | bytes 4980752 | tf_op jit(solution)/shard_map/reduce_scatter | solution.py:91
  227.0 4.1 convert_element_type.69
  231.1 4.5 all-to-all-start.4
  235.7 70.5 %all-gather.18.cloned.1.call-done = bf16[1536,1280]{1,0:T(8,128)(2,1)} async-done(((bf16[384,1280]{1,0:T(8,128)(2,1)}), bf16[1536,1280]{1,0:T(8,128)(2,1)}) %all-gather.18.cloned.1.call-update) | async-done | bytes 3932176 | tf_op jit(solution)/shard_map/all_gather | solution.py:15
  306.1 6.3 %copy.27 = bf16[384,4,1280]{0,2,1:T(8,128)(2,1)} copy(bf16[384,4,1280]{2,0,1:T(8,128)(2,1)} %bitcast.80) | data formatting | bytes 7864320 | tf_op jit(solution)/shard_map/reshape | solution.py:15
  312.4 2.9 slice.34
  315.4 3.5 slice.33
  318.9 68.4 %all-gather.14.cloned.1.call-done = bf16[2048,3584]{1,0:T(8,128)(2,1)} async-done(((bf16[256,3584]{1,0:T(8,128)(2,1)}), bf16[2048,3584]{1,0:T(8,128)(2,1)}) %all-gather.14.cloned.1.call-update) | async-done | bytes 14680080 | tf_op jit(solution)/shard_map/all_gather | solution.py:66
  387.3 9.4 %convolution_convert_fusion.1 = bf16[384,2048]{1,0:T(8,128)(2,1)S(1)} fusion(bf16[384,3584]{1,0:T(8,128)(2,1)S(1)} %copy-done, bf16[2048,3584]{1,0:T(8,128)(2,1)} %all-gather.14.cloned.1.call-done), kind=kOutput, calls=%fused_computation.9 | convolution fusion | flops 5637931008 | bytes 19005440 | tf_op jit(solution)/shard_map/dot_general | solution.py:22
  398.1 4.6 all-to-all-start.3
  402.7 3.1 reduce_sum.62
  405.8 95.9 %all-gather.12.cloned.1.call-done = bf16[3072,3584]{1,0:T(8,128)(2,1)} async-done(((bf16[384,3584]{1,0:T(8,128)(2,1)}), bf16[3072,3584]{1,0:T(8,128)(2,1)}) %all-gather.12.cloned.1.call-update) | async-done | bytes 22020112 | tf_op jit(solution)/shard_map/all_gather | solution.py:66
  501.7 14.1 %convolution_convert_fusion = bf16[384,3072]{1,0:T(8,128)(2,1)} fusion(bf16[384,3584]{1,0:T(8,128)(2,1)S(1)} %copy-done, bf16[3072,3584]{1,0:T(8,128)(2,1)} %all-gather.12.cloned.1.call-done), kind=kOutput, calls=%fused_computation.5 | convolution fusion | flops 8456896512 | bytes 27131904 | tf_op jit(solution)/shard_map/dot_general | solution.py:22
  515.8 3.2 copy.39
  519.0 4.8 all-to-all-start.2
  523.8 11.6 %fusion.9 = f32[384,3584]{1,0:T(8,128)} fusion(bf16[384,2048]{0,1:T(8,128)(2,1)S(1)} %bitcast.79, bf16[2048,3584]{1,0:T(8,128)(2,1)} %all-gather.14.cloned.1.call-done), kind=kOutput, calls=%fused_computation.34 | convolution fusion | flops 5637144576 | bytes 21757952 | tf_op jit(solution)/shard_map/dot_general | solution.py:110
  538.5 4.1 all-gather.16.cloned.1.call-done
  542.6 2.4 slice.36
  545.0 2.3 slice.37
  547.3 14.3 %fusion.8 = f32[384,3584]{1,0:T(8,128)S(1)} fusion(bf16[384,3072]{0,1:T(8,128)(2,1)S(1)} %bitcast.86, bf16[3072,3584]{1,0:T(8,128)(2,1)} %all-gather.12.cloned.1.call-done), kind=kOutput, calls=%fused_computation.33 | convolution fusion | flops 8455716864 | bytes 29884416 | tf_op jit(solution)/shard_map/dot_general | solution.py:110
  561.6 3.2 fusion.1
  564.8 13.3 %all-to-all-done.2 = bf16[4,384,768]{2,1,0:T(8,128)(2,1)} async-done(((bf16[4,384,768]{2,1,0:T(8,128)(2,1)}), bf16[4,384,768]{2,1,0:T(8,128)(2,1)}, u32[]{:S(2)}, u32[]{:S(2)}) %all-to-all-start.2) | async-done | bytes 2359328 | tf_op jit(solution)/shard_map/all_to_all | solution.py:102
  578.2 2.1 convert_reduce_fusion
  580.9 2.0 pad_maximum_fusion.1
  (63 shorter events, 22.4 us)
Async XLA Ops:
  7.2 131.5 %copy-start = (bf16[384,3584]{1,0:T(8,128)(2,1)S(1)}, bf16[384,3584]{1,0:T(8,128)(2,1)}, u32[]{:S(2)}) copy-start(bf16[384,3584]{1,0:T(8,128)(2,1)} %param.13) | copy-start | bytes 8257540
  17.4 33.8 %all-to-all-start = ((bf16[4,2,40960]{2,1,0:T(2,128)(2,1)}), bf16[4,2,40960]{2,1,0:T(2,128)(2,1)S(1)}, u32[]{:S(2)}, u32[]{:S(2)}) async-start(bf16[4,2,40960]{2,1,0:T(2,128)(2,1)} %reshape.172), calls=%async_computation | async-start | bytes 1310720 | tf_op jit(solution)/shard_map/all_to_all | solution.py:32
  51.3 47.2 %all-to-all-start.1 = ((bf16[4,2,114688]{2,1,0:T(2,128)(2,1)}), bf16[4,2,114688]{2,1,0:T(2,128)(2,1)}, u32[]{:S(2)}, u32[]{:S(2)}) async-start(bf16[4,2,114688]{2,1,0:T(2,128)(2,1)} %reshape.174), calls=%async_computation.1 | async-start | bytes 3670016 | tf_op jit(solution)/shard_map/all_to_all | solution.py:32
  56.4 70.5 %all-gather.8.cloned.1.call-start = ((), (), s32[]{:S(2)}) async-start(), calls=%async_computation.6 | async-start | bytes 1966080 | tf_op jit(solution)/shard_map/all_gather | solution.py:33
  66.1 72.6 %all-gather.10.cloned.1.call-start = ((), (), s32[]{:S(2)}) async-start(), calls=%async_computation.7 | async-start | bytes 5505024 | tf_op jit(solution)/shard_map/all_gather | solution.py:33
  123.4 3.1 copy-start.7
  123.4 3.1 copy-start.8
  126.5 60.1 %all-reduce.2.cloned.1.call-start = ((), (), s32[]{:S(2)}) async-start(), calls=%async_computation.8 | async-start | bytes 393216 | tf_op jit(solution)/shard_map/psum | solution.py:82
  150.3 76.7 %reduce-scatter.2.cloned.1.call-start = ((), (), s32[]{:S(2)}) async-start(), calls=%async_computation.11 | async-start | bytes 14942208 | tf_op jit(solution)/shard_map/reduce_scatter | solution.py:91
  209.6 96.6 %all-gather.18.cloned.1.call-start = ((), (), s32[]{:S(2)}) async-start(), calls=%async_computation.13 | async-start | bytes 4915200 | tf_op jit(solution)/shard_map/all_gather | solution.py:15
  210.2 177.2 %all-gather.14.cloned.1.call-start = ((), (), s32[]{:S(2)}) async-start(), calls=%async_computation.10 | async-start | bytes 16515072 | tf_op jit(solution)/shard_map/all_gather | solution.py:66
  213.1 288.6 %all-gather.12.cloned.1.call-start = ((), (), s32[]{:S(2)}) async-start(), calls=%async_computation.9 | async-start | bytes 24772608 | tf_op jit(solution)/shard_map/all_gather | solution.py:66
  231.1 166.9 %all-to-all-start.4 = ((bf16[4,64,4864]{2,1,0:T(8,128)(2,1)}), bf16[4,64,4864]{2,1,0:T(8,128)(2,1)}, u32[]{:S(2)}, u32[]{:S(2)}) async-start(bf16[4,64,4864]{2,1,0:T(8,128)(2,1)} %bitcast.73), calls=%async_computation.5 | async-start | bytes 4980736 | tf_op jit(solution)/shard_map/all_to_all | solution.py:38
  398.1 120.9 %all-to-all-start.3 = ((bf16[4,384,512]{2,1,0:T(8,128)(2,1)}), bf16[4,384,512]{2,1,0:T(8,128)(2,1)}, u32[]{:S(2)}, u32[]{:S(2)}) async-start(bf16[4,384,512]{2,1,0:T(8,128)(2,1)} %bitcast.78), calls=%async_computation.3 | async-start | bytes 3145728 | tf_op jit(solution)/shard_map/all_to_all | solution.py:102
  402.7 139.9 %all-gather.16.cloned.1.call-start = ((), (), s32[]{:S(2)}) async-start(), calls=%async_computation.12 | async-start | bytes 3112960 | tf_op jit(solution)/shard_map/all_gather | solution.py:42
  518.9 4.9 copy-start.3
  519.0 59.2 %all-to-all-start.2 = ((bf16[4,384,768]{2,1,0:T(8,128)(2,1)}), bf16[4,384,768]{2,1,0:T(8,128)(2,1)}, u32[]{:S(2)}, u32[]{:S(2)}) async-start(bf16[4,384,768]{2,1,0:T(8,128)(2,1)} %bitcast.62), calls=%async_computation.2 | async-start | bytes 4718592 | tf_op jit(solution)/shard_map/all_to_all | solution.py:102
  542.6 2.4 copy-start.2
  545.0 2.3 copy-start.5
  545.0 16.6 %slice-start = ((s8[5505024]{0:T(1024)(128)(4,1)}), s8[4194304]{0:T(1024)(128)(4,1)S(1)}, s32[]{:S(2)}) async-start(s8[5505024]{0:T(1024)(128)(4,1)} %bitcast.65), calls=%async_computation.14 | async-start | bytes 8388608
  547.3 14.3 %slice-start.1 = ((s8[5505024]{0:T(1024)(128)(4,1)}), s8[1310720]{0:T(1024)(128)(4,1)S(1)}, s32[]{:S(2)}) async-start(s8[5505024]{0:T(1024)(128)(4,1)} %bitcast.65), calls=%async_computation.15 | async-start | bytes 2621440
  547.3 14.3 %copy-start.4 = (bf16[8,64,3584]{2,1,0:T(8,128)(2,1)S(1)}, bf16[8,64,3584]{2,1,0:T(8,128)(2,1)}, u32[]{:S(2)}) copy-start(bf16[8,64,3584]{2,1,0:T(8,128)(2,1)} %all-gather.10.cloned.1.call-done) | copy-start | bytes 11010052
  582.9 1.3 copy-start.6
  582.9 2.9 copy-start.1
Sparse Core Ops, SparseCore 0:
  66.2 10.8 all-gather.7
  126.7 11.9 all-gather.9
  150.4 36.1 all-reduce.1
  209.7 17.2 reduce-scatter.1
  228.4 77.6 all-gather.17
  307.9 79.3 all-gather.13
  389.8 111.8 all-gather.11
  504.1 38.4 all-gather.15
